TPU v7x, 32 devices: a whole 2x2x4 slice. The times are simulated.
32 devices in a mesh: tp: 8 (over z, y), kv: 4 (over x, core).
Axes of the slice: x: 2, y: 2, z: 4, core: 2. Of those that a mesh axis runs over, the one named last changes fastest.
Arguments:
- hidden_in: bfloat16 [2048, 4096], P(('kv', 'tp')), may hold values from -6 to 6
- gain_attn: float32 [4096], replicated, may hold values from 0.4 to 1.6
- w_qkv: bfloat16 [4096, 32, 384], P(None, 'tp'), may hold values from -0.09375 to 0.09375
- cache_kv: bfloat16 [2, 8192, 32, 256], P(None, 'kv', 'tp'), may hold values from -110 to 110
- cache_len: int32 [2], replicated, may hold values from 128 to 8192, as said below
- w_out: bfloat16 [4096, 4096], P('tp'), may hold values from -0.1875 to 0.1875
- gain_mlp: float32 [4096], replicated, may hold values from 0.1 to 1.9
- w_gate_up: bfloat16 [4096, 2, 11008], P('kv', None, 'tp'), may hold values from -0.09375 to 0.09375
- w_down: bfloat16 [11008, 4096], P('tp', 'kv'), may hold values from -0.0546875 to 0.0546875
Outputs:
- layer_out: bfloat16 [2048, 4096], P(('kv', 'tp'))
Inputs may be any that keep to these rules, and one draw needn't show every extreme that they name: `cache_len`: every length is a multiple of 128; some sequence uses the whole cache.
All inputs are finite; a program needn't handle non-finite values.
Results may differ from a plain program's by a relative error of at most 0.019.
The roundings to bfloat16 on the way count: a program that leaves them out, or rounds other values in their place, can miss the bound.
Values may be sent and summed in bfloat16 or wider, within the bound.
A program may use at most 192 MiB of HBM per device.

v0:
```python
import math
import jax
import jax.numpy as jnp
from jax import lax
from jax.sharding import PartitionSpec as P

EPSILON = 1e-05
MASKED = -1e30


def rms_scale(values_in, gain_vector):
    widened = values_in.astype(jnp.float32)
    mean_square = jnp.mean(widened * widened, axis=-1, keepdims=True)
    return (widened * lax.rsqrt(mean_square + EPSILON) * gain_vector).astype(jnp.bfloat16)


def per_device(
    hidden_in, gain_attn, w_qkv, cache_kv, cache_len, w_out, gain_mlp, w_gate_up, w_down
):
    local_heads = w_qkv.shape[1]
    head_dim = w_qkv.shape[2] // 3
    own_rows = hidden_in.shape[0]
    block_input = lax.all_gather(hidden_in, "tp", axis=0, tiled=True)
    block_rows = block_input.shape[0]
    normed = rms_scale(block_input, gain_attn)
    flat_qkv = w_qkv.reshape(w_qkv.shape[0], local_heads * 3 * head_dim)
    packed = jnp.dot(normed, flat_qkv, preferred_element_type=jnp.float32).astype(jnp.bfloat16)
    packed = packed.reshape(block_rows, local_heads, 3 * head_dim)
    key_mine = packed[:, :, head_dim : 2 * head_dim]
    value_mine = packed[:, :, 2 * head_dim :]
    query_rows = lax.all_gather(packed[:, :, :head_dim], "kv", axis=0, tiled=True)
    seq_count = cache_kv.shape[0]
    span_len = query_rows.shape[0] // seq_count
    kv_index = lax.axis_index("kv")
    cache_rows = cache_kv.shape[1]
    cache_pos = kv_index * cache_rows + jnp.arange(cache_rows, dtype=jnp.int32)
    own_seq = (kv_index * block_rows + jnp.arange(block_rows, dtype=jnp.int32)) // span_len
    row_peaks, masses, accums = ([], [], [])
    for seq_id in range(seq_count):
        query_block = query_rows[seq_id * span_len : (seq_id + 1) * span_len]
        joined_key_rows = jnp.concatenate([cache_kv[seq_id, :, :, :head_dim], key_mine], axis=0)
        joined_value_rows = jnp.concatenate([cache_kv[seq_id, :, :, head_dim:], value_mine], axis=0)
        usable = jnp.concatenate([cache_pos < cache_len[seq_id], own_seq == seq_id])
        logit_scores = jnp.einsum(
            "qhd,khd->hqk", query_block, joined_key_rows, preferred_element_type=jnp.float32
        ) / math.sqrt(head_dim)
        logit_scores = jnp.where(usable[None, None, :], logit_scores, MASKED)
        row_peak = jnp.max(logit_scores, axis=2)
        raw_weights = jnp.where(
            usable[None, None, :], jnp.exp(logit_scores - row_peak[:, :, None]), 0.0
        )
        row_peaks.append(row_peak.T)
        masses.append(jnp.sum(raw_weights, axis=2).T)
        accums.append(
            jnp.einsum(
                "hqk,khd->qhd",
                raw_weights.astype(jnp.bfloat16),
                joined_value_rows,
                preferred_element_type=jnp.float32,
            )
        )
    peak_all = jnp.concatenate(row_peaks, axis=0)
    mass_all = jnp.concatenate(masses, axis=0)
    accum_all = jnp.concatenate(accums, axis=0)
    peak_set, mass_set, accum_set = (
        lax.all_to_all(peak_all[None], "kv", split_axis=1, concat_axis=0, tiled=True),
        lax.all_to_all(mass_all[None], "kv", split_axis=1, concat_axis=0, tiled=True),
        lax.all_to_all(accum_all[None], "kv", split_axis=1, concat_axis=0, tiled=True),
    )
    peak_best = jnp.max(peak_set, axis=0)
    scaling = jnp.exp(peak_set - peak_best[None])
    mass_own = jnp.sum(mass_set * scaling, axis=0)
    accum_own = jnp.sum(accum_set * scaling[..., None], axis=0)
    attended = (
        (accum_own / mass_own[..., None])
        .astype(jnp.bfloat16)
        .reshape(block_rows, local_heads * head_dim)
    )
    tp_index = lax.axis_index("tp")
    heads_sum = lax.psum(
        jnp.dot(attended, w_out, preferred_element_type=jnp.float32).astype(jnp.bfloat16), "tp"
    ).astype(jnp.float32)
    residual = block_input.astype(jnp.float32) + heads_sum
    mlp_in = rms_scale(residual, gain_mlp)
    residual_own = lax.dynamic_slice_in_dim(residual, tp_index * own_rows, own_rows, 0)
    gate_up = jnp.einsum(
        "td,dgf->tgf",
        mlp_in,
        lax.all_gather(w_gate_up, "kv", axis=0, tiled=True),
        preferred_element_type=jnp.float32,
    )
    activated = (jax.nn.silu(gate_up[:, 0, :]) * gate_up[:, 1, :]).astype(jnp.bfloat16)
    down_terms = jnp.dot(
        activated,
        lax.all_gather(w_down, "kv", axis=1, tiled=True),
        preferred_element_type=jnp.float32,
    )
    down_own = lax.psum_scatter(
        down_terms.astype(jnp.bfloat16), "tp", scatter_dimension=0, tiled=True
    ).astype(jnp.float32)
    return (residual_own + down_own).astype(jnp.bfloat16)


def solution(mesh):
    in_specs = (
        P(("kv", "tp"), None),
        P(),
        P(None, "tp", None),
        P(None, "kv", "tp", None),
        P(),
        P("tp", None),
        P(),
        P("kv", None, "tp"),
        P("tp", "kv"),
    )
    out_specs = P(("kv", "tp"), None)
    return jax.shard_map(
        per_device, mesh=mesh, in_specs=in_specs, out_specs=out_specs, check_vma=False
    )
```

profile of v0, /device:TPU:0, one launch (start us, length us, event | category | flops | bytes accessed | tf_op | source)
XLA Modules:
  0.0 827.3 jit_solution(16002876231132787441)
XLA Ops:
  7.3 12.4 %copy.51 = bf16[512,8,4,384]{3,1,2,0:T(8,128)(2,1)} copy(bf16[512,8,4,384]{3,2,1,0:T(4,128)(2,1)} %bitcast.50) | data formatting | bytes 25165824
  19.7 65.3 %all-gather.5.cloned.1.call-done = bf16[512,4096]{1,0:T(8,128)(2,1)} async-done(((bf16[64,4096]{1,0:T(8,128)(2,1)}), bf16[512,4096]{1,0:T(8,128)(2,1)}) %all-gather.5.cloned.1.call-update) | async-done | bytes 4194320 | tf_op jit(solution)/shard_map/all_gather | solution.py:23
  85.0 3.1 fusion.12
  88.1 11.0 %fusion.24 = bf16[512,1536]{1,0:T(8,128)(2,1)S(1)} fusion(bf16[4096,1536]{1,0:T(8,128)(2,1)} %bitcast.51, bf16[512,4096]{1,0:T(8,128)(2,1)} %all-gather.5.cloned.1.call-done, f32[4096]{0:T(1024)S(1)} %copy-done.5, f32[512]{0:T(512)S(1)} %add_rsqrt_fusion.1), kind=kOutput, calls=%fused_computation.37 | convolution fusion | flops 6451625984 | bytes 18368512 | tf_op jit(solution)/shard_map/dot_general | solution.py:27
  100.9 6.4 fusion.61
  107.4 4.4 copy.44
  111.8 2.6 copy.49
  116.3 4.1 copy_bitcast_fusion
  122.2 19.7 %fusion.1 = (f32[4,1024]{1,0:T(4,128)S(1)}, f32[4,1024,2560]{2,1,0:T(8,128)}) fusion(pred[2560]{0:T(1024)(128)(4,1)S(1)} %pad_add_fusion.1, bf16[512,4,128]{2,0,1:T(8,128)(2,1)S(1)} %copy.48, bf16[2048,4,128]{2,0,1:T(8,128)(2,1)} %get-tuple-element.26, bf16[2048,4,128]{2,0,1:T(8,128)(2,1)} %all-gather.7.cloned.1.call-done), kind=kOutput, calls=%fused_computation.5 | convolution fusion | flops 2721050624 | bytes 45632000 | tf_op jit(solution)/shard_map/qhd,khd->hqk/dot_general | solution.py:44
  141.8 19.2 %fusion.4 = f32[4,1024]{1,0:T(4,128)S(1)} fusion(f32[4,1024,2560]{2,1,0:T(8,128)} %get-tuple-element.19, f32[4,1024]{1,0:T(4,128)S(1)} %get-tuple-element.18, pred[2560]{0:T(1024)(128)(4,1)S(1)} %pad_add_fusion.1), kind=kLoop, calls=%fused_computation.8 | loop fusion | flops 52424704 | bytes 41978368 | tf_op jit(solution)/shard_map/reduce_sum | solution.py:53
  161.1 17.9 %fusion.38 = f32[1024,4,128]{0,2,1:T(8,128)} fusion(f32[4,1024,2560]{2,1,0:T(8,128)} %get-tuple-element.19, f32[4,1024]{1,0:T(4,128)S(1)} %get-tuple-element.18, pred[2560]{0:T(1024)(128)(4,1)S(1)} %pad_add_fusion.1, bf16[512,4,128]{0,2,1:T(8,128)(2,1)S(1)} %copy-done.3, bf16[2048,4,128]{0,2,1:T(8,128)(2,1)S(1)} %bitcast.59), kind=kOutput, calls=%fused_computation.51 | convolution fusion | flops 2742026240 | bytes 46680576 | tf_op jit(solution)/shard_map/hqk,khd->qhd/dot_general | solution.py:55
  178.9 19.0 %fusion = (f32[4,1024]{1,0:T(4,128)S(1)}, f32[4,1024,2560]{2,1,0:T(8,128)}) fusion(pred[2560]{0:T(1024)(128)(4,1)S(1)} %pad_add_fusion, bf16[512,4,128]{2,0,1:T(8,128)(2,1)S(1)} %copy.48, bf16[2048,4,128]{2,0,1:T(8,128)(2,1)S(1)} %get-tuple-element.27, bf16[2048,4,128]{2,0,1:T(8,128)(2,1)} %all-gather.7.cloned.1.call-done), kind=kOutput, calls=%fused_computation.4 | convolution fusion | flops 2721050624 | bytes 45632000 | tf_op jit(solution)/shard_map/qhd,khd->hqk/dot_general | solution.py:44
  198.0 19.2 %fusion.2 = f32[4,1024]{1,0:T(4,128)S(1)} fusion(f32[4,1024,2560]{2,1,0:T(8,128)} %get-tuple-element.21, f32[4,1024]{1,0:T(4,128)S(1)} %get-tuple-element.20, pred[2560]{0:T(1024)(128)(4,1)S(1)} %pad_add_fusion), kind=kLoop, calls=%fused_computation.6 | loop fusion | flops 52424704 | bytes 41978368 | tf_op jit(solution)/shard_map/reduce_sum | solution.py:53
  217.2 17.9 %fusion.35 = f32[1024,4,128]{0,2,1:T(8,128)} fusion(f32[4,1024,2560]{2,1,0:T(8,128)} %get-tuple-element.21, f32[4,1024]{1,0:T(4,128)S(1)} %get-tuple-element.20, pred[2560]{0:T(1024)(128)(4,1)S(1)} %pad_add_fusion, bf16[512,4,128]{0,2,1:T(8,128)(2,1)S(1)} %copy-done.3, bf16[2048,4,128]{0,2,1:T(8,128)(2,1)S(1)} %bitcast.58), kind=kOutput, calls=%fused_computation.50 | convolution fusion | flops 2742026240 | bytes 46680576 | tf_op jit(solution)/shard_map/hqk,khd->qhd/dot_general | solution.py:55
  236.1 9.5 %reduce.2 = f32[2048,4]{1,0:T(8,128)S(1)} reduce(f32[2048,1,4]{2,1,0:T(1,128)S(1)} %bitcast.54, f32[]{:T(128)} %broadcast.98), dimensions={1}, to_apply=%bitcast.41.reduce_sub_computation | reduce | bytes 65540
  247.0 3.3 all-to-all-start.1
  250.6 9.3 %reduce = f32[2048,4]{1,0:T(8,128)S(1)} reduce(f32[2048,1,4]{2,1,0:T(1,128)S(1)} %bitcast.55, f32[]{:T(128)} %broadcast.98), dimensions={1}, to_apply=%bitcast.43.reduce_sub_computation | reduce | bytes 65540
  261.3 3.3 all-to-all-start.2
  264.6 4.6 maximum_bitcast_fusion
  269.2 5.2 copy.37
  274.5 4.9 all-to-all-start
  285.5 42.0 %all-to-all-done = f32[1,2048,4,128]{3,2,0,1:T(4,128)} async-done(((f32[1,2048,4,128]{3,2,0,1:T(4,128)}), f32[1,2048,4,128]{3,2,0,1:T(4,128)}, u32[]{:S(2)}, u32[]{:S(2)}) %all-to-all-start) | async-done | bytes 4194336 | tf_op jit(solution)/shard_map/all_to_all | solution.py:68
  327.5 5.3 copy.41
  332.9 5.1 multiply_reduce_fusion.1
  338.1 4.5 convolution_convert_fusion.1
  344.1 155.1 %all-reduce.2.cloned.1.call-done = bf16[512,4096]{1,0:T(8,128)(2,1)} async-done(((bf16[512,4096]{1,0:T(8,128)(2,1)}), bf16[512,4096]{1,0:T(8,128)(2,1)}) %all-reduce.2.cloned.1.call-update) | async-done | bytes 4194320 | tf_op jit(solution)/shard_map/psum | solution.py:80
  499.2 9.2 %convert_add_fusion = (f32[512,4096]{1,0:T(8,128)}, f32[512]{0:T(512)S(1)}) fusion(bf16[512,4096]{1,0:T(8,128)(2,1)} %all-gather.5.cloned.1.call-done, bf16[512,4096]{1,0:T(8,128)(2,1)} %all-reduce.2.cloned.1.call-done), kind=kLoop, calls=%fused_computation.14 | loop fusion | flops 10485248 | bytes 16779264 | tf_op jit(solution)/shard_map/add | solution.py:83
  508.4 131.6 %all-gather.9.cloned.1.call-done = bf16[4096,2,1376]{0,2,1:T(8,128)(2,1)} async-done(((bf16[1024,2,1376]{0,2,1:T(8,128)(2,1)}), bf16[4096,2,1376]{0,2,1:T(8,128)(2,1)}) %all-gather.9.cloned.1.call-update) | async-done | bytes 22544400 | tf_op jit(solution)/shard_map/all_gather | solution.py:89
  639.9 20.5 %fusion.16 = f32[512,2,1376]{0,2,1:T(8,128)} fusion(bf16[4096,2,1376]{0,2,1:T(8,128)(2,1)} %all-gather.9.cloned.1.call-done, f32[4096]{0:T(1024)S(1)} %copy-done.6, f32[512]{0:T(512)S(1)} %add_rsqrt_fusion, bf16[512,4096]{1,0:T(8,128)(2,1)} %all-gather.5.cloned.1.call-done, bf16[512,4096]{1,0:T(8,128)(2,1)} %all-reduce.2.cloned.1.call-done), kind=kOutput, calls=%fused_computation.25 | convolution fusion | flops 11555307520 | bytes 36587520 | tf_op jit(solution)/shard_map/td,dgf->tgf/dot_general | solution.py:86
  660.4 55.6 %all-gather.11.cloned.1.call-done = bf16[1376,4096]{1,0:T(8,128)(2,1)} async-done(((bf16[1376,1024]{1,0:T(8,128)(2,1)}), bf16[1376,4096]{1,0:T(8,128)(2,1)}) %all-gather.11.cloned.1.call-update) | async-done | bytes 11272208 | tf_op jit(solution)/shard_map/all_gather | solution.py:95
  716.0 13.6 %convolution_convert_fusion = bf16[512,4096]{1,0:T(8,128)(2,1)} fusion(bf16[1376,4096]{1,0:T(8,128)(2,1)} %all-gather.11.cloned.1.call-done, f32[512,2,1376]{0,2,1:T(8,128)} %fusion.16), kind=kOutput, calls=%fused_computation.22 | convolution fusion | flops 5777686528 | bytes 21102592 | tf_op jit(solution)/shard_map/dot_general | solution.py:93
  729.6 88.4 %reduce-scatter.2.cloned.1.call-done = bf16[64,4096]{1,0:T(8,128)(2,1)} async-done(((bf16[512,4096]{1,0:T(8,128)(2,1)}), bf16[64,4096]{1,0:T(8,128)(2,1)}) %reduce-scatter.2.cloned.1.call-update) | async-done | bytes 524304 | tf_op jit(solution)/shard_map/reduce_scatter | solution.py:98
  (59 shorter events, 20.2 us)
Async XLA Ops:
  6.5 78.5 %all-gather.5.cloned.1.call-start = ((), (), s32[]{:S(2)}) async-start(), calls=%async_computation.4 | async-start | bytes 4718592 | tf_op jit(solution)/shard_map/all_gather | solution.py:23
  7.3 114.9 %all-gather.7.cloned.1.call-start = ((), (), s32[]{:S(2)}) async-start(), calls=%async_computation.5 | async-start | bytes 2621440 | tf_op jit(solution)/shard_map/all_gather | solution.py:31
  7.3 80.8 %copy-start.5 = (f32[4096]{0:T(1024)S(1)}, f32[4096]{0:T(1024)}, u32[]{:S(2)}) copy-start(f32[4096]{0:T(1024)} %param.10) | copy-start | bytes 49156
  107.4 7.1 copy-start.4
  141.8 19.2 %copy-start.2 = (bf16[1,2048,4,128]{1,3,2,0:T(8,128)(2,1)S(1)}, bf16[1,2048,4,128]{1,3,2,0:T(8,128)(2,1)}, u32[]{:S(2)}) copy-start(bf16[1,2048,4,128]{1,3,2,0:T(8,128)(2,1)} %copy.49) | copy-start | bytes 6291460
  141.8 19.2 %copy-start.3 = (bf16[512,4,128]{0,2,1:T(8,128)(2,1)S(1)}, bf16[512,4,128]{0,2,1:T(8,128)(2,1)}, u32[]{:S(2)}) copy-start(bf16[512,4,128]{0,2,1:T(8,128)(2,1)} %copy.45) | copy-start | bytes 1572868
  198.0 19.2 %copy-start.1 = (bf16[1,2048,4,128]{1,3,2,0:T(8,128)(2,1)S(1)}, bf16[1,2048,4,128]{1,3,2,0:T(8,128)(2,1)}, u32[]{:S(2)}) copy-start(bf16[1,2048,4,128]{1,3,2,0:T(8,128)(2,1)} %copy.44) | copy-start | bytes 6291460
  247.0 14.4 %all-to-all-start.1 = ((f32[4,1,2048]{2,1,0:T(1,128)}), f32[4,1,2048]{2,1,0:T(1,128)S(1)}, u32[]{:S(2)}, u32[]{:S(2)}) async-start(f32[4,1,2048]{2,1,0:T(1,128)} %reshape.59), calls=%async_computation.1 | async-start | bytes 65536 | tf_op jit(solution)/shard_map/all_to_all | solution.py:66
  261.3 13.2 %all-to-all-start.2 = ((f32[4,1,2048]{2,1,0:T(1,128)}), f32[4,1,2048]{2,1,0:T(1,128)S(1)}, u32[]{:S(2)}, u32[]{:S(2)}) async-start(f32[4,1,2048]{2,1,0:T(1,128)} %reshape.61), calls=%async_computation.2 | async-start | bytes 65536 | tf_op jit(solution)/shard_map/all_to_all | solution.py:67
  274.5 53.1 %all-to-all-start = ((f32[1,2048,4,128]{3,2,0,1:T(4,128)}), f32[1,2048,4,128]{3,2,0,1:T(4,128)}, u32[]{:S(2)}, u32[]{:S(2)}) async-start(f32[1,2048,4,128]{3,2,0,1:T(4,128)} %copy.37), calls=%async_computation | async-start | bytes 8388608 | tf_op jit(solution)/shard_map/all_to_all | solution.py:68
  279.3 219.8 %all-reduce.2.cloned.1.call-start = ((), (), s32[]{:S(2)}) async-start(), calls=%async_computation.6 | async-start | bytes 8388608 | tf_op jit(solution)/shard_map/psum | solution.py:80
  332.9 5.3 copy-start
  342.7 297.3 %all-gather.9.cloned.1.call-start = ((), (), s32[]{:S(2)}) async-start(), calls=%async_computation.7 | async-start | bytes 28180480 | tf_op jit(solution)/shard_map/all_gather | solution.py:89
  343.2 372.8 %all-gather.11.cloned.1.call-start = ((), (), s32[]{:S(2)}) async-start(), calls=%async_computation.8 | async-start | bytes 14090240 | tf_op jit(solution)/shard_map/all_gather | solution.py:95
  343.8 296.1 %copy-start.6 = (f32[4096]{0:T(1024)S(1)}, f32[4096]{0:T(1024)}, u32[]{:S(2)}) copy-start(f32[4096]{0:T(1024)} %param.15) | copy-start | bytes 49156
  343.8 474.2 %reduce-scatter.2.cloned.1.call-start = ((), (), s32[]{:S(2)}) async-start(), calls=%async_computation.9 | async-start | bytes 4718592 | tf_op jit(solution)/shard_map/reduce_scatter | solution.py:98
Sparse Core Ops, SparseCore 0:
  9.5 75.5 all-gather.4
  101.0 21.0 all-gather.6
  342.8 156.3 all-reduce.1
  500.6 139.2 all-gather.8
  641.3 74.6 all-gather.10
  729.7 88.2 reduce-scatter.1
where the time goes:
time: 835 us; the launch traced here: 827 us
  waiting for transfers between devices  540 us (65%)
  matrix products  124 us (15%)
  other arithmetic  84.6 us (10%)
  local copies, waits for them, and re-layouts  52.2 us (6%)
  between operations  13.9 us (2%)
  starting transfers between devices  12.2 us (1%)
    psum x1, waiting for transfers between devices, per_device(): lax.psum(jnp.dot(attended, w_out, preferred_element_type=jnp.float32).ast...  155 us
    all_gather x1, waiting for transfers between devices, per_device(): lax.all_gather(w_gate_up, 'kv', axis=0, tiled=True)  132 us
    reduce_scatter x1, waiting for transfers between devices, per_device(): lax.psum_scatter(down_terms.astype(jnp.bfloat16), 'tp', scatter_dimension...  88.4 us
    all_gather x1, waiting for transfers between devices, per_device(): block_input = lax.all_gather(hidden_in, 'tp', axis=0, tiled=True)  65.3 us
    all_gather x1, waiting for transfers between devices, per_device(): lax.all_gather(w_down, 'kv', axis=1, tiled=True)  55.6 us
    all_to_all x1, waiting for transfers between devices, per_device(): lax.all_to_all(accum_all[None], 'kv', split_axis=1, concat_axis=0, tiled=...  42 us
    dot_general x2, matrix products, per_device(): jnp.einsum('qhd,khd->hqk', query_block, joined_key_rows, preferred_elemen...  38.7 us
    reduce_sum x2, other arithmetic, per_device(): masses.append(jnp.sum(raw_weights, axis=2).T)  38.4 us
  transfers between devices with their start and end apart: 9, of which 7 were waited for; matrix products, arithmetic and copies ran while one was open for 11% of the time, Pallas kernels for 0%

commit v1 on v0

--- a/solution.py
+++ b/solution.py
@@ -92,7 +92,7 @@
     activated = (jax.nn.silu(gate_up[:, 0, :]) * gate_up[:, 1, :]).astype(jnp.bfloat16)
     down_terms = jnp.dot(
         activated,
-        lax.all_gather(w_down, "kv", axis=1, tiled=True),
+        jnp.concatenate(lax.all_gather(w_down, "kv"), axis=1),
         preferred_element_type=jnp.float32,
     )
     down_own = lax.psum_scatter(

time: 835 us -> 778 us (0.932)
  waiting for transfers between devices: 540 us -> 470 us
  local copies, waits for them, and re-layouts: 52.2 us -> 67.9 us
    all_gather x1, waiting for transfers between devices: 55.6 us -> 0.02 us  [per_device(): lax.all_gather(w_down, 'kv')]
    all_gather x0 -> x1, local copies, waits for them, and re-layouts: none -> 15.6 us  [per_device(): lax.all_gather(w_down, 'kv')]
    psum x1, waiting for transfers between devices: 155 us -> 140 us  [per_device(): lax.psum(jnp.dot(attended, w_out, preferred_element_type=jnp.float32).ast...]
    unnamed x25 -> x23, local copies, waits for them, and re-layouts: 28.1 us -> 28.1 us
  transfers between devices with their start and end apart: 9 -> 9, of which waited for: 7 -> 5; matrix products, arithmetic and copies ran while one was open for 11% -> 29% of each run, Pallas kernels for 0% -> 0%
where the time goes in v1:
time: 778 us; the launch traced here: 772 us
  waiting for transfers between devices  470 us (60%)
  matrix products  125 us (16%)
  other arithmetic  84 us (11%)
  local copies, waits for them, and re-layouts  67.9 us (9%)
  between operations  14 us (2%)
  starting transfers between devices  11.6 us (1%)
    psum x1, waiting for transfers between devices, per_device(): lax.psum(jnp.dot(attended, w_out, preferred_element_type=jnp.float32).ast...  140 us
    all_gather x1, waiting for transfers between devices, per_device(): lax.all_gather(w_gate_up, 'kv', axis=0, tiled=True)  132 us
    reduce_scatter x1, waiting for transfers between devices, per_device(): lax.psum_scatter(down_terms.astype(jnp.bfloat16), 'tp', scatter_dimension...  88.4 us
    all_gather x1, waiting for transfers between devices, per_device(): block_input = lax.all_gather(hidden_in, 'tp', axis=0, tiled=True)  65.3 us
    all_to_all x1, waiting for transfers between devices, per_device(): lax.all_to_all(accum_all[None], 'kv', split_axis=1, concat_axis=0, tiled=...  42.6 us
    dot_general x2, matrix products, per_device(): jnp.einsum('qhd,khd->hqk', query_block, joined_key_rows, preferred_elemen...  42.4 us
    reduce_sum x2, other arithmetic, per_device(): masses.append(jnp.sum(raw_weights, axis=2).T)  38.1 us
    dot_general x2, matrix products, per_device(): jnp.einsum('hqk,khd->qhd', raw_weights.astype(jnp.bfloat16), joined_value...  36.1 us
  transfers between devices with their start and end apart: 9, of which 5 were waited for; matrix products, arithmetic and copies ran while one was open for 29% of the time, Pallas kernels for 0%

profile of v1, /device:TPU:0, one launch (start us, length us, event | category | flops | bytes accessed | tf_op | source)
XLA Modules:
  0.0 772.3 jit_solution(5645785185996065027)
XLA Ops:
  7.3 12.4 %copy.61 = bf16[512,8,4,384]{3,1,2,0:T(8,128)(2,1)} copy(bf16[512,8,4,384]{3,2,1,0:T(4,128)(2,1)} %bitcast.45) | data formatting | bytes 25165824
  19.7 65.3 %all-gather.6.cloned.1.call-done = bf16[512,4096]{1,0:T(8,128)(2,1)} async-done(((bf16[64,4096]{1,0:T(8,128)(2,1)}), bf16[512,4096]{1,0:T(8,128)(2,1)}) %all-gather.6.cloned.1.call-update) | async-done | bytes 4194320 | tf_op jit(solution)/shard_map/all_gather | solution.py:23
  85.0 3.1 fusion.12
  88.1 11.2 %fusion.24 = bf16[512,1536]{1,0:T(8,128)(2,1)S(1)} fusion(bf16[4096,1536]{1,0:T(8,128)(2,1)} %bitcast.46, bf16[512,4096]{1,0:T(8,128)(2,1)} %all-gather.6.cloned.1.call-done, f32[4096]{0:T(1024)S(1)} %copy-done.4, f32[512]{0:T(512)S(1)} %add_rsqrt_fusion.1), kind=kOutput, calls=%fused_computation.37 | convolution fusion | flops 6451625984 | bytes 18368512 | tf_op jit(solution)/shard_map/dot_general | solution.py:27
  102.6 6.6 fusion.60
  109.1 4.4 copy.54
  113.5 2.7 copy.59
  117.4 4.1 copy_bitcast_fusion
  122.8 22.9 %fusion.1 = (f32[4,1024]{1,0:T(4,128)S(1)}, f32[4,1024,2560]{2,1,0:T(8,128)}) fusion(pred[2560]{0:T(1024)(128)(4,1)S(1)} %pad_add_fusion.1, bf16[512,4,128]{2,0,1:T(8,128)(2,1)S(1)} %copy.58, bf16[2048,4,128]{2,0,1:T(8,128)(2,1)} %get-tuple-element.26, bf16[2048,4,128]{2,0,1:T(8,128)(2,1)} %all-gather.8.cloned.1.call-done), kind=kOutput, calls=%fused_computation.5 | convolution fusion | flops 2721050624 | bytes 45632000 | tf_op jit(solution)/shard_map/qhd,khd->hqk/dot_general | solution.py:44
  145.7 19.5 %fusion = (f32[4,1024]{1,0:T(4,128)S(1)}, f32[4,1024,2560]{2,1,0:T(8,128)}) fusion(pred[2560]{0:T(1024)(128)(4,1)S(1)} %pad_add_fusion, bf16[512,4,128]{2,0,1:T(8,128)(2,1)S(1)} %copy.58, bf16[2048,4,128]{2,0,1:T(8,128)(2,1)S(1)} %get-tuple-element.27, bf16[2048,4,128]{2,0,1:T(8,128)(2,1)} %all-gather.8.cloned.1.call-done), kind=kOutput, calls=%fused_computation.4 | convolution fusion | flops 2721050624 | bytes 45632000 | tf_op jit(solution)/shard_map/qhd,khd->hqk/dot_general | solution.py:44
  166.1 9.3 %reduce.2 = f32[2048,4]{1,0:T(8,128)S(1)} reduce(f32[2048,1,4]{2,1,0:T(1,128)S(1)} %bitcast.51, f32[]{:T(128)} %broadcast.100), dimensions={1}, to_apply=%bitcast.36.reduce_sub_computation | reduce | bytes 65540
  176.7 3.3 all-to-all-start.1
  180.0 18.2 %fusion.37 = f32[1024,4,128]{0,2,1:T(8,128)} fusion(f32[4,1024,2560]{2,1,0:T(8,128)} %get-tuple-element.19, f32[4,1024]{1,0:T(4,128)S(1)} %get-tuple-element.18, pred[2560]{0:T(1024)(128)(4,1)S(1)} %pad_add_fusion.1, bf16[512,4,128]{0,2,1:T(8,128)(2,1)S(1)} %copy-done.2, bf16[2048,4,128]{0,2,1:T(8,128)(2,1)} %bitcast.56), kind=kOutput, calls=%fused_computation.49 | convolution fusion | flops 2742026240 | bytes 46680576 | tf_op jit(solution)/shard_map/hqk,khd->qhd/dot_general | solution.py:55
  198.2 17.9 %fusion.34 = f32[1024,4,128]{0,2,1:T(8,128)} fusion(f32[4,1024,2560]{2,1,0:T(8,128)} %get-tuple-element.21, f32[4,1024]{1,0:T(4,128)S(1)} %get-tuple-element.20, pred[2560]{0:T(1024)(128)(4,1)S(1)} %pad_add_fusion, bf16[512,4,128]{0,2,1:T(8,128)(2,1)S(1)} %copy-done.2, bf16[2048,4,128]{0,2,1:T(8,128)(2,1)S(1)} %bitcast.55), kind=kOutput, calls=%fused_computation.48 | convolution fusion | flops 2742026240 | bytes 46680576 | tf_op jit(solution)/shard_map/hqk,khd->qhd/dot_general | solution.py:55
  216.1 19.0 %fusion.4 = f32[4,1024]{1,0:T(4,128)S(1)} fusion(f32[4,1024,2560]{2,1,0:T(8,128)} %get-tuple-element.19, f32[4,1024]{1,0:T(4,128)S(1)} %get-tuple-element.18, pred[2560]{0:T(1024)(128)(4,1)S(1)} %pad_add_fusion.1), kind=kLoop, calls=%fused_computation.8 | loop fusion | flops 52424704 | bytes 41978368 | tf_op jit(solution)/shard_map/reduce_sum | solution.py:53
  235.2 19.1 %fusion.2 = f32[4,1024]{1,0:T(4,128)S(1)} fusion(f32[4,1024,2560]{2,1,0:T(8,128)} %get-tuple-element.21, f32[4,1024]{1,0:T(4,128)S(1)} %get-tuple-element.20, pred[2560]{0:T(1024)(128)(4,1)S(1)} %pad_add_fusion), kind=kLoop, calls=%fused_computation.6 | loop fusion | flops 52424704 | bytes 41978368 | tf_op jit(solution)/shard_map/reduce_sum | solution.py:53
  254.6 9.4 %reduce = f32[2048,4]{1,0:T(8,128)S(1)} reduce(f32[2048,1,4]{2,1,0:T(1,128)S(1)} %bitcast.52, f32[]{:T(128)} %broadcast.100), dimensions={1}, to_apply=%bitcast.38.reduce_sub_computation | reduce | bytes 65540
  265.4 3.3 all-to-all-start.2
  268.7 4.6 maximum_bitcast_fusion
  273.4 5.2 copy.46
  278.6 4.9 all-to-all-start
  289.1 42.6 %all-to-all-done = f32[1,2048,4,128]{3,2,0,1:T(4,128)} async-done(((f32[1,2048,4,128]{3,2,0,1:T(4,128)}), f32[1,2048,4,128]{3,2,0,1:T(4,128)}, u32[]{:S(2)}, u32[]{:S(2)}) %all-to-all-start) | async-done | bytes 4194336 | tf_op jit(solution)/shard_map/all_to_all | solution.py:68
  331.6 5.3 copy.50
  337.0 5.1 multiply_reduce_fusion.1
  342.2 4.5 convolution_convert_fusion.1
  347.4 15.6 %copy.53 = bf16[4,1376,1024]{1,2,0:T(8,128)(2,1)} copy(bf16[4,1376,1024]{2,1,0:T(8,128)(2,1)} %bitcast.48) | data formatting | bytes 22544384 | tf_op jit(solution)/shard_map/all_gather | solution.py:95
  363.0 140.0 %all-reduce.2.cloned.1.call-done = bf16[512,4096]{1,0:T(8,128)(2,1)} async-done(((bf16[512,4096]{1,0:T(8,128)(2,1)}), bf16[512,4096]{1,0:T(8,128)(2,1)}) %all-reduce.2.cloned.1.call-update) | async-done | bytes 4194320 | tf_op jit(solution)/shard_map/psum | solution.py:80
  503.0 9.2 %convert_add_fusion = (f32[512,4096]{1,0:T(8,128)}, f32[512]{0:T(512)S(1)}) fusion(bf16[512,4096]{1,0:T(8,128)(2,1)} %all-gather.6.cloned.1.call-done, bf16[512,4096]{1,0:T(8,128)(2,1)} %all-reduce.2.cloned.1.call-done), kind=kLoop, calls=%fused_computation.14 | loop fusion | flops 10485248 | bytes 16779264 | tf_op jit(solution)/shard_map/add | solution.py:83
  512.2 131.5 %all-gather.10.cloned.1.call-done = bf16[4096,2,1376]{0,2,1:T(8,128)(2,1)} async-done(((bf16[1024,2,1376]{0,2,1:T(8,128)(2,1)}), bf16[4096,2,1376]{0,2,1:T(8,128)(2,1)}) %all-gather.10.cloned.1.call-update) | async-done | bytes 22544400 | tf_op jit(solution)/shard_map/all_gather | solution.py:89
  643.8 18.0 %fusion.16 = f32[512,2,1376]{0,2,1:T(8,128)S(1)} fusion(bf16[4096,2,1376]{0,2,1:T(8,128)(2,1)} %all-gather.10.cloned.1.call-done, f32[4096]{0:T(1024)S(1)} %copy-done.5, f32[512]{0:T(512)S(1)} %add_rsqrt_fusion, bf16[512,4096]{1,0:T(8,128)(2,1)} %all-gather.6.cloned.1.call-done, bf16[512,4096]{1,0:T(8,128)(2,1)} %all-reduce.2.cloned.1.call-done), kind=kOutput, calls=%fused_computation.25 | convolution fusion | flops 11555307520 | bytes 36587520 | tf_op jit(solution)/shard_map/td,dgf->tgf/dot_general | solution.py:86
  661.7 12.7 %convolution_convert_fusion = bf16[512,4096]{1,0:T(8,128)(2,1)} fusion(bf16[1376,4096]{0,1:T(8,128)(2,1)} %bitcast.47, f32[512,2,1376]{0,2,1:T(8,128)S(1)} %fusion.16), kind=kOutput, calls=%fused_computation.22 | convolution fusion | flops 5777686528 | bytes 21102592 | tf_op jit(solution)/shard_map/dot_general | solution.py:93
  674.5 88.4 %reduce-scatter.2.cloned.1.call-done = bf16[64,4096]{1,0:T(8,128)(2,1)} async-done(((bf16[512,4096]{1,0:T(8,128)(2,1)}), bf16[64,4096]{1,0:T(8,128)(2,1)}) %reduce-scatter.2.cloned.1.call-update) | async-done | bytes 524304 | tf_op jit(solution)/shard_map/reduce_scatter | solution.py:98
  (58 shorter events, 19.1 us)
Async XLA Ops:
  6.5 78.5 %all-gather.6.cloned.1.call-start = ((), (), s32[]{:S(2)}) async-start(), calls=%async_computation.4 | async-start | bytes 4718592 | tf_op jit(solution)/shard_map/all_gather | solution.py:23
  7.3 115.5 %all-gather.8.cloned.1.call-start = ((), (), s32[]{:S(2)}) async-start(), calls=%async_computation.5 | async-start | bytes 2621440 | tf_op jit(solution)/shard_map/all_gather | solution.py:31
  7.3 80.8 %copy-start.4 = (f32[4096]{0:T(1024)S(1)}, f32[4096]{0:T(1024)}, u32[]{:S(2)}) copy-start(f32[4096]{0:T(1024)} %param.10) | copy-start | bytes 49156
  99.3 2.6 copy-start.3
  101.2 246.3 %all-gather.12.cloned.1.call-start = ((), (), s32[]{:S(2)}) async-start(), calls=%async_computation.9 | async-start | bytes 14090240 | tf_op jit(solution)/shard_map/all_gather | solution.py:95
  145.7 34.3 %copy-start.2 = (bf16[512,4,128]{0,2,1:T(8,128)(2,1)S(1)}, bf16[512,4,128]{0,2,1:T(8,128)(2,1)}, u32[]{:S(2)}) copy-start(bf16[512,4,128]{0,2,1:T(8,128)(2,1)} %copy.55) | copy-start | bytes 1572868
  176.7 88.7 %all-to-all-start.1 = ((f32[4,1,2048]{2,1,0:T(1,128)}), f32[4,1,2048]{2,1,0:T(1,128)S(1)}, u32[]{:S(2)}, u32[]{:S(2)}) async-start(f32[4,1,2048]{2,1,0:T(1,128)} %reshape.69), calls=%async_computation.1 | async-start | bytes 65536 | tf_op jit(solution)/shard_map/all_to_all | solution.py:66
  180.0 18.2 %copy-start.1 = (bf16[1,2048,4,128]{1,3,2,0:T(8,128)(2,1)S(1)}, bf16[1,2048,4,128]{1,3,2,0:T(8,128)(2,1)}, u32[]{:S(2)}) copy-start(bf16[1,2048,4,128]{1,3,2,0:T(8,128)(2,1)} %copy.54) | copy-start | bytes 6291460
  265.4 13.2 %all-to-all-start.2 = ((f32[4,1,2048]{2,1,0:T(1,128)}), f32[4,1,2048]{2,1,0:T(1,128)S(1)}, u32[]{:S(2)}, u32[]{:S(2)}) async-start(f32[4,1,2048]{2,1,0:T(1,128)} %reshape.71), calls=%async_computation.2 | async-start | bytes 65536 | tf_op jit(solution)/shard_map/all_to_all | solution.py:67
  278.6 53.1 %all-to-all-start = ((f32[1,2048,4,128]{3,2,0,1:T(4,128)}), f32[1,2048,4,128]{3,2,0,1:T(4,128)}, u32[]{:S(2)}, u32[]{:S(2)}) async-start(f32[1,2048,4,128]{3,2,0,1:T(4,128)} %copy.46), calls=%async_computation | async-start | bytes 8388608 | tf_op jit(solution)/shard_map/all_to_all | solution.py:68
  283.4 219.6 %all-reduce.2.cloned.1.call-start = ((), (), s32[]{:S(2)}) async-start(), calls=%async_computation.6 | async-start | bytes 8388608 | tf_op jit(solution)/shard_map/psum | solution.py:80
  337.0 5.3 copy-start
  346.8 297.0 %all-gather.10.cloned.1.call-start = ((), (), s32[]{:S(2)}) async-start(), calls=%async_computation.7 | async-start | bytes 28180480 | tf_op jit(solution)/shard_map/all_gather | solution.py:89
  347.4 415.5 %reduce-scatter.2.cloned.1.call-start = ((), (), s32[]{:S(2)}) async-start(), calls=%async_computation.8 | async-start | bytes 4718592 | tf_op jit(solution)/shard_map/reduce_scatter | solution.py:98
  363.0 280.8 %copy-start.5 = (f32[4096]{0:T(1024)S(1)}, f32[4096]{0:T(1024)}, u32[]{:S(2)}) copy-start(f32[4096]{0:T(1024)} %param.15) | copy-start | bytes 49156
Sparse Core Ops, SparseCore 0:
  9.5 75.5 all-gather.5
  101.3 21.0 all-gather.7
  124.0 74.9 all-gather.11
  346.9 156.0 all-reduce.1
  504.4 139.2 all-gather.9
  674.6 88.2 reduce-scatter.1
